TPU v7x, 1024 devices: a whole 8x8x8 slice. The times are simulated.
1024 devices in a mesh: fsdp: 64 (over y, x_hi, core), dp: 16 (over z, x_lo).
Axes of the slice: x: 8 (x_hi: 4, x_lo: 2; x = x_hi * 2 + x_lo), y: 8, z: 8, core: 2. Of those that a mesh axis runs over, the one named last changes fastest.
Arguments:
- inputs: bfloat16 [262144, 2560], P(('fsdp', 'dp')), may hold values from -24 to 24
- value_cotangent: bfloat16 [262144, 512], P(('fsdp', 'dp')), may hold values from -0.03125 to 0.03125
- master: float32 [2560, 4, 128], P('fsdp', None, 'dp'), may hold values from -0.125 to 0.125
- first_moment: float32 [2560, 4, 128], P('fsdp', None, 'dp'), may hold values from -6 to 6
- second_moment: float32 [2560, 4, 128], P('fsdp', None, 'dp'), may hold values from 0.25 to 4
Outputs:
- moment_one_new: float32 [2560, 4, 128], P('fsdp', None, 'dp')
- moment_two_new: float32 [2560, 4, 128], P('fsdp', None, 'dp')
- master_new: float32 [2560, 4, 128], P('fsdp', None, 'dp')
- head_blocks: bfloat16 [64, 2560, 128], P('fsdp', None, 'dp')
All inputs are finite; a program needn't handle non-finite values.
Results may differ from a plain program's by a relative error of at most 0.0018.
Values may be sent and summed in bfloat16 or wider, within the bound.
No kernel may reach another device: no remote copies, remote signals or barrier semaphores. Data moves between devices by JAX's collectives and lax.ppermute only.
A program may use at most 32 MiB of HBM per device.

v0:
```python
import jax
import jax.numpy as jnp
from jax import lax
from jax.sharding import PartitionSpec as P

KVH = 4
HEAD = 128
STEP = 8


beta_first = 0.9
beta_second = 0.95
learn_rate = 0.001
weight_decay = 0.1
epsilon = 1e-08


def in_blocks(x, dim, devices):
    before, after = (x.shape[:dim], x.shape[dim + 1 :])
    return jnp.moveaxis(x.reshape(*before, devices, -1, *after), dim, 0)


def summed_on_arrival(x, axis, dim):
    devices = lax.axis_size(axis)
    tiles = lax.all_to_all(in_blocks(x, dim, devices), axis, 0, 0, tiled=True)
    return jnp.sum(tiles.astype(jnp.float32), axis=0)


def summed_on_arrival_2(x, axis, dim):
    tiles = in_blocks(x, dim, lax.axis_size(axis))
    arrived = lax.all_to_all(tiles, axis, split_axis=0, concat_axis=0, tiled=True)
    return arrived.sum(axis=0)


def adam_update(gradient, moment_one, moment_two, weights):
    moment_one_new = beta_first * moment_one + (1.0 - beta_first) * gradient
    moment_two_new = beta_second * moment_two + (1.0 - beta_second) * gradient * gradient
    correct_one = 1.0 - beta_first**STEP
    correct_two = 1.0 - beta_second**STEP
    update = (
        moment_one_new / correct_one / (jnp.sqrt(moment_two_new / correct_two) + epsilon)
        + weight_decay * weights
    )
    return (moment_one_new, moment_two_new, weights - learn_rate * update)


def shards(inputs, value_cotangent, master, first_moment, second_moment):
    slice_width = master.shape[2]
    head_parts = []
    for head in range(KVH):
        head_cot = value_cotangent[:, head * HEAD : (head + 1) * HEAD]
        head_term = lax.dot_general(
            inputs, head_cot, (((0,), (0,)), ((), ())), preferred_element_type=jnp.float32
        )
        head_parts.append(summed_on_arrival(head_term.astype(jnp.bfloat16), "dp", 1))
    column_part = jnp.stack(head_parts, axis=1)
    grad_share = summed_on_arrival_2(column_part, "fsdp", 0)
    moment_one_new, moment_two_new, master_new = adam_update(
        grad_share, first_moment, second_moment, master
    )
    narrow_weight = master_new.astype(jnp.bfloat16)
    by_head = jnp.transpose(narrow_weight, (1, 0, 2))
    outgoing = jnp.tile(by_head, (lax.axis_size("fsdp") // KVH, 1, 1))
    arrived = lax.all_to_all(outgoing, "fsdp", split_axis=0, concat_axis=0, tiled=True)
    tp_block = arrived.reshape(1, -1, slice_width)
    return (moment_one_new, moment_two_new, master_new, tp_block)


def solution(mesh):
    placed = (
        P(("fsdp", "dp"), None),
        P(("fsdp", "dp"), None),
        P("fsdp", None, "dp"),
        P("fsdp", None, "dp"),
        P("fsdp", None, "dp"),
    )
    return jax.shard_map(
        shards,
        mesh=mesh,
        in_specs=placed,
        out_specs=(
            P("fsdp", None, "dp"),
            P("fsdp", None, "dp"),
            P("fsdp", None, "dp"),
            P("fsdp", None, "dp"),
        ),
        check_vma=False,
    )
```

profile of v0, /device:TPU:1, one launch (start us, length us, event | category | flops | bytes accessed | tf_op | source)
XLA Modules:
  0.0 164.4 jit_solution(6900328017505900857)
XLA Ops:
  0.6 0.0 copy-start
  0.6 0.0 copy-start.1
  0.7 1.3 copy-done
  2.0 2.1 %fusion = bf16[16,2560,8]{1,2,0:T(8,128)(2,1)} fusion(bf16[256,2560]{1,0:T(8,128)(2,1)S(1)} %copy-done, bf16[256,512]{1,0:T(8,128)(2,1)} %param.6), kind=kOutput, calls=%fused_computation.4 | convolution fusion | flops 168099840 | bytes 2031616 | tf_op jit(solution)/shard_map/dot_general | solution.py:52
  4.0 18.3 %all-to-all-start = ((bf16[16,2560,8]{1,2,0:T(8,128)(2,1)}), bf16[16,2560,8]{1,2,0:T(8,128)(2,1)S(1)}, u32[]{:S(2)}, u32[]{:S(2)}) async-start(bf16[16,2560,8]{1,2,0:T(8,128)(2,1)} %fusion), calls=%async_computation | async-start | bytes 1310720 | tf_op jit(solution)/shard_map/all_to_all | solution.py:25
  22.3 0.0 copy-done.1
  22.3 1.2 fusion.1
  23.5 16.8 %all-to-all-done = bf16[16,2560,8]{1,2,0:T(8,128)(2,1)S(1)} async-done(((bf16[16,2560,8]{1,2,0:T(8,128)(2,1)}), bf16[16,2560,8]{1,2,0:T(8,128)(2,1)S(1)}, u32[]{:S(2)}, u32[]{:S(2)}) %all-to-all-start) | async-done | bytes 655392 | tf_op jit(solution)/shard_map/all_to_all | solution.py:25
  40.3 5.2 %all-to-all-start.1 = ((bf16[16,2560,8]{1,2,0:T(8,128)(2,1)}), bf16[16,2560,8]{1,2,0:T(8,128)(2,1)S(1)}, u32[]{:S(2)}, u32[]{:S(2)}) async-start(bf16[16,2560,8]{1,2,0:T(8,128)(2,1)} %fusion.1), calls=%async_computation.1 | async-start | bytes 1310720 | tf_op jit(solution)/shard_map/all_to_all | solution.py:25
  45.5 1.2 fusion.2
  46.8 16.8 %all-to-all-done.1 = bf16[16,2560,8]{1,2,0:T(8,128)(2,1)S(1)} async-done(((bf16[16,2560,8]{1,2,0:T(8,128)(2,1)}), bf16[16,2560,8]{1,2,0:T(8,128)(2,1)S(1)}, u32[]{:S(2)}, u32[]{:S(2)}) %all-to-all-start.1) | async-done | bytes 655392 | tf_op jit(solution)/shard_map/all_to_all | solution.py:25
  63.6 5.2 %all-to-all-start.2 = ((bf16[16,2560,8]{1,2,0:T(8,128)(2,1)}), bf16[16,2560,8]{1,2,0:T(8,128)(2,1)S(1)}, u32[]{:S(2)}, u32[]{:S(2)}) async-start(bf16[16,2560,8]{1,2,0:T(8,128)(2,1)} %fusion.2), calls=%async_computation.2 | async-start | bytes 1310720 | tf_op jit(solution)/shard_map/all_to_all | solution.py:25
  68.8 1.2 fusion.3
  70.0 16.8 %all-to-all-done.2 = bf16[16,2560,8]{1,2,0:T(8,128)(2,1)S(1)} async-done(((bf16[16,2560,8]{1,2,0:T(8,128)(2,1)}), bf16[16,2560,8]{1,2,0:T(8,128)(2,1)S(1)}, u32[]{:S(2)}, u32[]{:S(2)}) %all-to-all-start.2) | async-done | bytes 655392 | tf_op jit(solution)/shard_map/all_to_all | solution.py:25
  86.8 5.2 %all-to-all-start.3 = ((bf16[16,2560,8]{1,2,0:T(8,128)(2,1)}), bf16[16,2560,8]{1,2,0:T(8,128)(2,1)}, u32[]{:S(2)}, u32[]{:S(2)}) async-start(bf16[16,2560,8]{1,2,0:T(8,128)(2,1)} %fusion.3), calls=%async_computation.3 | async-start | bytes 1310720 | tf_op jit(solution)/shard_map/all_to_all | solution.py:25
  92.1 0.1 convert_reduce_fusion.3
  92.1 0.2 stack.15
  92.3 0.1 convert_reduce_fusion.2
  92.4 0.2 stack.16
  92.6 0.1 convert_reduce_fusion.1
  92.7 0.2 stack.17
  92.9 17.2 %all-to-all-done.3 = bf16[16,2560,8]{1,2,0:T(8,128)(2,1)} async-done(((bf16[16,2560,8]{1,2,0:T(8,128)(2,1)}), bf16[16,2560,8]{1,2,0:T(8,128)(2,1)}, u32[]{:S(2)}, u32[]{:S(2)}) %all-to-all-start.3) | async-done | bytes 655392 | tf_op jit(solution)/shard_map/all_to_all | solution.py:25
  110.1 1.2 convert_reduce_fusion
  111.3 0.2 stack.18
  111.5 0.1 pad_maximum_fusion
  111.6 0.6 copy.26
  112.2 1.0 reshape.41
  113.2 29.5 %all_to_all.30 = f32[64,1,1280]{2,1,0:T(1,128)S(1)} all-to-all(f32[64,1,1280]{2,1,0:T(1,128)S(1)} %reshape.41), channel_id=1, replica_groups=mesh['fsdp'=64,'dp'=16] {'fsdp'}, dimensions={0} | all-to-all | bytes 655360 | tf_op jit(solution)/shard_map/all_to_all | solution.py:31
  142.7 0.5 broadcast.13
  143.2 1.4 reduce
  144.7 0.0 copy-start.2
  144.7 0.0 copy-start.3
  144.7 0.0 copy-start.4
  144.7 0.8 reshape.42
  145.5 0.1 bitcast_reduce_fusion
  145.6 0.0 copy-done.2
  145.6 0.0 copy-done.3
  145.6 0.0 copy-done.4
  145.6 0.6 convert_bitcast_fusion
  146.3 0.2 reshape.43
  146.5 17.0 %all_to_all.31 = bf16[64,2,160]{2,1,0:T(2,128)(2,1)S(1)} all-to-all(bf16[64,2,160]{2,1,0:T(2,128)(2,1)S(1)} %reshape.43), channel_id=1, replica_groups=mesh['fsdp'=64,'dp'=16] {'fsdp'}, dimensions={0} | all-to-all | bytes 81920 | tf_op jit(solution)/shard_map/all_to_all | solution.py:64
  163.4 0.1 reshape.44
  163.6 0.8 reshape.40
  (2 shorter events, 0.0 us)
Async XLA Ops:
  0.6 1.3 copy-start
  0.6 21.7 %copy-start.1 = (bf16[256,512]{1,0:T(8,128)(2,1)S(1)}, bf16[256,512]{1,0:T(8,128)(2,1)}, u32[]{:S(2)}) copy-start(bf16[256,512]{1,0:T(8,128)(2,1)} %param.6) | copy-start | bytes 786436
  4.0 36.3 %all-to-all-start = ((bf16[16,2560,8]{1,2,0:T(8,128)(2,1)}), bf16[16,2560,8]{1,2,0:T(8,128)(2,1)S(1)}, u32[]{:S(2)}, u32[]{:S(2)}) async-start(bf16[16,2560,8]{1,2,0:T(8,128)(2,1)} %fusion), calls=%async_computation | async-start | bytes 1310720 | tf_op jit(solution)/shard_map/all_to_all | solution.py:25
  40.3 23.3 %all-to-all-start.1 = ((bf16[16,2560,8]{1,2,0:T(8,128)(2,1)}), bf16[16,2560,8]{1,2,0:T(8,128)(2,1)S(1)}, u32[]{:S(2)}, u32[]{:S(2)}) async-start(bf16[16,2560,8]{1,2,0:T(8,128)(2,1)} %fusion.1), calls=%async_computation.1 | async-start | bytes 1310720 | tf_op jit(solution)/shard_map/all_to_all | solution.py:25
  63.6 23.2 %all-to-all-start.2 = ((bf16[16,2560,8]{1,2,0:T(8,128)(2,1)}), bf16[16,2560,8]{1,2,0:T(8,128)(2,1)S(1)}, u32[]{:S(2)}, u32[]{:S(2)}) async-start(bf16[16,2560,8]{1,2,0:T(8,128)(2,1)} %fusion.2), calls=%async_computation.2 | async-start | bytes 1310720 | tf_op jit(solution)/shard_map/all_to_all | solution.py:25
  86.8 23.3 %all-to-all-start.3 = ((bf16[16,2560,8]{1,2,0:T(8,128)(2,1)}), bf16[16,2560,8]{1,2,0:T(8,128)(2,1)}, u32[]{:S(2)}, u32[]{:S(2)}) async-start(bf16[16,2560,8]{1,2,0:T(8,128)(2,1)} %fusion.3), calls=%async_computation.3 | async-start | bytes 1310720 | tf_op jit(solution)/shard_map/all_to_all | solution.py:25
  144.7 1.0 copy-start.2
  144.7 1.0 copy-start.3
  144.7 1.0 copy-start.4
where the time goes:
time: 166 us; the launch traced here: 164 us
  waiting for transfers between devices  67.5 us (41%)
  blocking collectives  46.5 us (28%)
  starting transfers between devices  33.9 us (20%)
  local copies, waits for them, and re-layouts  6.11 us (4%)
  matrix products  5.77 us (3%)
  other arithmetic  3.69 us (2%)
    all_to_all x4, waiting for transfers between devices, summed_on_arrival(): tiles = lax.all_to_all(in_blocks(x, dim, devices), axis, 0, 0, tiled=True)  67.5 us
    all_to_all x4, starting transfers between devices, summed_on_arrival(): tiles = lax.all_to_all(in_blocks(x, dim, devices), axis, 0, 0, tiled=True)  33.9 us
    all_to_all x1, blocking collectives, summed_on_arrival_2(): lax.all_to_all(tiles, axis, split_axis=0, concat_axis=0, tiled=True)  29.5 us
    all_to_all x1, blocking collectives, shards(): lax.all_to_all(outgoing, 'fsdp', split_axis=0, concat_axis=0, tiled=True)  17 us
    dot_general x4, matrix products, shards(): lax.dot_general(inputs, head_cot, (((0,), (0,)), ((), ())), preferred_ele...  5.77 us
    unnamed x14, local copies, waits for them, and re-layouts  3.39 us
  transfers between devices with their start and end apart: 4, of which 4 were waited for; matrix products, arithmetic and copies ran while one was open for 3% of the time, Pallas kernels for 0%

commit v1 on v0

--- a/solution.py
+++ b/solution.py
@@ -26,12 +26,6 @@
     return jnp.sum(tiles.astype(jnp.float32), axis=0)
 
 
-def summed_on_arrival_2(x, axis, dim):
-    tiles = in_blocks(x, dim, lax.axis_size(axis))
-    arrived = lax.all_to_all(tiles, axis, split_axis=0, concat_axis=0, tiled=True)
-    return arrived.sum(axis=0)
-
-
 def adam_update(gradient, moment_one, moment_two, weights):
     moment_one_new = beta_first * moment_one + (1.0 - beta_first) * gradient
     moment_two_new = beta_second * moment_two + (1.0 - beta_second) * gradient * gradient
@@ -46,15 +40,12 @@
 
 def shards(inputs, value_cotangent, master, first_moment, second_moment):
     slice_width = master.shape[2]
-    head_parts = []
-    for head in range(KVH):
-        head_cot = value_cotangent[:, head * HEAD : (head + 1) * HEAD]
-        head_term = lax.dot_general(
-            inputs, head_cot, (((0,), (0,)), ((), ())), preferred_element_type=jnp.float32
-        )
-        head_parts.append(summed_on_arrival(head_term.astype(jnp.bfloat16), "dp", 1))
-    column_part = jnp.stack(head_parts, axis=1)
-    grad_share = summed_on_arrival_2(column_part, "fsdp", 0)
+    term = lax.dot_general(
+        inputs, value_cotangent, (((0,), (0,)), ((), ())), preferred_element_type=jnp.float32
+    )
+    term = term.astype(jnp.bfloat16).reshape(-1, KVH, HEAD)
+    column_part = summed_on_arrival(term, "dp", 2)
+    grad_share = summed_on_arrival(column_part.astype(jnp.bfloat16), "fsdp", 0)
     moment_one_new, moment_two_new, master_new = adam_update(
         grad_share, first_moment, second_moment, master
     )

time: 166 us -> 135 us (0.81)
  blocking collectives: 46.5 us -> 123 us
  waiting for transfers between devices: 67.5 us -> 0 us
  starting transfers between devices: 33.9 us -> 0 us
  matrix products: 5.77 us -> 1.83 us
    all_to_all x1 -> x2, blocking collectives: 29.5 us -> 107 us  [summed_on_arrival(): tiles = lax.all_to_all(in_blocks(x, dim, devices), axis, 0, 0, tiled=True)]
    all_to_all x4 -> x0, waiting for transfers between devices: 67.5 us -> none  [summed_on_arrival(): tiles = lax.all_to_all(in_blocks(x, dim, devices), axis, 0, 0, tiled=True)]
    all_to_all x4 -> x0, starting transfers between devices: 33.9 us -> none  [summed_on_arrival(): tiles = lax.all_to_all(in_blocks(x, dim, devices), axis, 0, 0, tiled=True)]
    dot_general x4 -> x1, matrix products: 5.77 us -> 1.83 us  [shards(): lax.dot_general(inputs, value_cotangent, (((0,), (0,)), ((), ())), prefer...]
    unnamed x14 -> x12, local copies, waits for them, and re-layouts: 3.39 us -> 3.18 us
  transfers between devices with their start and end apart: 4 -> 0, of which waited for: 4 -> 0; matrix products, arithmetic and copies ran while one was open for 3% -> 0% of each run, Pallas kernels for 0% -> 0%
where the time goes in v1:
time: 135 us; the launch traced here: 134 us
  blocking collectives  123 us (91%)
  local copies, waits for them, and re-layouts  5.54 us (4%)
  other arithmetic  2.91 us (2%)
  matrix products  1.83 us (1%)
    all_to_all x2, blocking collectives, summed_on_arrival(): tiles = lax.all_to_all(in_blocks(x, dim, devices), axis, 0, 0, tiled=True)  107 us
    all_to_all x1, blocking collectives, shards(): lax.all_to_all(outgoing, 'fsdp', split_axis=0, concat_axis=0, tiled=True)  16.1 us
    unnamed x12, local copies, waits for them, and re-layouts  3.18 us

profile of v1, /device:TPU:1, one launch (start us, length us, event | category | flops | bytes accessed | tf_op | source)
XLA Modules:
  0.0 134.4 jit_solution(308930980898535173)
XLA Ops:
  0.6 0.0 copy-start
  0.6 1.3 copy-done
  2.0 1.8 %convolution_convert_fusion = bf16[2560,512]{0,1:T(8,128)(2,1)S(1)} fusion(bf16[256,2560]{1,0:T(8,128)(2,1)S(1)} %copy-done, bf16[256,512]{1,0:T(8,128)(2,1)} %param.6), kind=kOutput, calls=%fused_computation | convolution fusion | flops 672399360 | bytes 4194304 | tf_op jit(solution)/shard_map/dot_general | solution.py:43
  3.8 0.3 copy.22
  4.1 78.0 %all_to_all.15 = bf16[16,2560,4,8]{1,3,2,0:T(8,128)(2,1)} all-to-all(bf16[16,2560,4,8]{1,3,2,0:T(8,128)(2,1)S(1)} %bitcast.21), channel_id=1, replica_groups=mesh['fsdp'=64,'dp'=16] {'dp'}, dimensions={0} | all-to-all | bytes 5242880 | tf_op jit(solution)/shard_map/all_to_all | solution.py:25
  82.0 2.1 %reduce_sum.21 = bf16[2560,4,8]{0,2,1:T(8,128)(2,1)S(1)} reduce(bf16[16,2560,4,8]{1,3,2,0:T(8,128)(2,1)} %all_to_all.15, bf16[]{:T(256)} %constant.4.clone.1), dimensions={0}, to_apply=%region_0.0 | reduce | flops 1228800 | bytes 2785282 | tf_op jit(solution)/shard_map/reduce_sum | solution.py:26
  84.2 0.0 copy-start.1
  84.2 0.0 copy-start.2
  84.2 0.0 copy-start.3
  84.2 0.9 reshape.18
  85.1 0.3 copy.23
  85.5 0.8 reshape.20
  86.3 29.3 %all_to_all.16 = bf16[64,2,640]{2,1,0:T(2,128)(2,1)S(1)} all-to-all(bf16[64,2,640]{2,1,0:T(2,128)(2,1)S(1)} %reshape.20), channel_id=1, replica_groups=mesh['fsdp'=64,'dp'=16] {'fsdp'}, dimensions={0} | all-to-all | bytes 327680 | tf_op jit(solution)/shard_map/all_to_all | solution.py:25
  115.6 0.8 reshape.21
  116.4 0.1 convert_reduce_fusion
  116.5 0.0 copy-done.1
  116.5 0.0 copy-done.2
  116.5 0.0 copy-done.3
  116.5 0.6 convert_bitcast_fusion
  117.2 0.2 reshape.22
  117.3 16.1 %all_to_all.17 = bf16[64,2,160]{2,1,0:T(2,128)(2,1)S(1)} all-to-all(bf16[64,2,160]{2,1,0:T(2,128)(2,1)S(1)} %reshape.22), channel_id=1, replica_groups=mesh['fsdp'=64,'dp'=16] {'fsdp'}, dimensions={0} | all-to-all | bytes 81920 | tf_op jit(solution)/shard_map/all_to_all | solution.py:55
  133.4 0.1 reshape.23
  133.6 0.8 reshape.19
  (2 shorter events, 0.0 us)
Async XLA Ops:
  0.6 1.3 copy-start
  84.2 32.3 %copy-start.1 = (f32[40,4,8]{0,2,1:T(8,128)S(1)}, f32[40,4,8]{0,2,1:T(8,128)}, u32[]{:S(2)}) copy-start(f32[40,4,8]{0,2,1:T(8,128)} %param.7) | copy-start | bytes 15364
  84.2 32.3 %copy-start.2 = (f32[40,4,8]{0,2,1:T(8,128)S(1)}, f32[40,4,8]{0,2,1:T(8,128)}, u32[]{:S(2)}) copy-start(f32[40,4,8]{0,2,1:T(8,128)} %param.9) | copy-start | bytes 15364
  84.2 32.3 %copy-start.3 = (f32[40,4,8]{0,2,1:T(8,128)S(1)}, f32[40,4,8]{0,2,1:T(8,128)}, u32[]{:S(2)}) copy-start(f32[40,4,8]{0,2,1:T(8,128)} %param.8) | copy-start | bytes 15364

commit v2 on v1

v2 whole, which is shorter than its diff:
```python
import math

import jax
import jax.numpy as jnp
from jax import lax
from jax.experimental import pallas as pl
from jax.experimental.pallas import tpu as pltpu
from jax.sharding import Mesh
from jax.sharding import PartitionSpec as P

KVH = 4
HEAD = 128
STEP = 8
LANES = 128

beta_first = 0.9
beta_second = 0.95
learn_rate = 0.001
weight_decay = 0.1
epsilon = 1e-08

VMEM = pl.BlockSpec(memory_space=pltpu.VMEM)
SMEM = pl.BlockSpec(memory_space=pltpu.SMEM)


def one_hot(test):
    return jnp.where(test, 1.0, 0.0)


def column_order(z_hi, z_lo, x_lo):
    width = KVH * HEAD
    share = HEAD // (z_hi * z_lo * x_lo)
    old = lax.broadcasted_iota(jnp.int32, (width, width), 0)
    new = lax.broadcasted_iota(jnp.int32, (width, width), 1)
    j = new % share
    head = new // share % KVH
    zh = new // (share * KVH) % z_hi
    xl = new // (share * KVH * z_hi) % x_lo
    zl = new // (share * KVH * z_hi * x_lo)
    source = head * HEAD + ((zh * z_lo + zl) * x_lo + xl) * share + j
    return one_hot(old == source).astype(jnp.bfloat16)


def partial_kernel(sizes, rows, which, core_ref, x_ref, cot_ref, out_ref, acc):
    z_hi, z_lo, x_lo = sizes
    order = column_order(z_hi, z_lo, x_lo)
    cot = jnp.dot(cot_ref[...], order, preferred_element_type=jnp.float32).astype(jnp.bfloat16)
    parity = core_ref[0] if which == "keep" else 1 - core_ref[0]
    d_in = x_ref.shape[1]
    chunk = 640
    pairs = chunk // (2 * rows)
    for c in range(d_in // chunk):
        acc[...] = lax.dot_general(
            x_ref[:, c * chunk : (c + 1) * chunk],
            cot,
            (((0,), (0,)), ((), ())),
            preferred_element_type=jnp.float32,
        )
        for k in range(pairs):
            start = pl.multiple_of((2 * k + parity) * rows, 8)
            block = acc[pl.ds(start, rows), :]
            at = (c * pairs + k) * rows
            for b in range(z_lo * x_lo):
                out_ref[b, at : at + rows, :] = block[:, b * LANES : (b + 1) * LANES].astype(out_ref.dtype)


def partials(which, sizes, rows, core, x, cot):
    d_in = x.shape[1]
    blocks = sizes[1] * sizes[2]
    dtype = jnp.float32 if which == "keep" else jnp.bfloat16
    return pl.pallas_call(
        lambda *refs: partial_kernel(sizes, rows, which, *refs),
        out_shape=jax.ShapeDtypeStruct((blocks, d_in // 2, LANES), dtype),
        in_specs=[SMEM, VMEM, VMEM],
        out_specs=VMEM,
        scratch_shapes=[pltpu.VMEM((640, KVH * HEAD), jnp.float32)],
        cost_estimate=pl.CostEstimate(flops=2 * x.shape[0] * d_in * KVH * HEAD, bytes_accessed=3 << 20, transcendentals=0),
        name="partial_" + which,
    )(core, x, cot)


def regroup_kernel(z_hi, parts_ref, out_ref, acc):
    total = parts_ref[0].astype(jnp.float32)
    for k in range(1, parts_ref.shape[0]):
        total = total + parts_ref[k].astype(jnp.float32)
    acc[...] = total
    n = acc.shape[0] // z_hi
    width = LANES // z_hi
    lane = lax.broadcasted_iota(jnp.int32, (n, LANES), 1) // width
    quarters = [acc[pl.ds(q, n, stride=z_hi), :] for q in range(z_hi)]
    for zh in range(z_hi):
        out = jnp.zeros((n, LANES), jnp.float32)
        for q in range(z_hi):
            shift = (q - zh) * width % LANES
            moved = quarters[q] if shift == 0 else pltpu.roll(quarters[q], shift, 1)
            out = jnp.where(lane == q, moved, out)
        out_ref[zh] = out.astype(out_ref.dtype)


def regroup(parts, z_hi):
    rows = parts.shape[1]
    return pl.pallas_call(
        lambda *refs: regroup_kernel(z_hi, *refs),
        out_shape=jax.ShapeDtypeStruct((z_hi, rows // z_hi, LANES), jnp.bfloat16),
        in_specs=[VMEM],
        out_specs=VMEM,
        scratch_shapes=[pltpu.VMEM((rows, LANES), jnp.float32)],
        name="regroup",
    )(parts)


def adam_update(gradient, moment_one, moment_two, weights):
    moment_one_new = beta_first * moment_one + (1.0 - beta_first) * gradient
    moment_two_new = beta_second * moment_two + (1.0 - beta_second) * gradient * gradient
    correct_one = 1.0 - beta_first**STEP
    correct_two = 1.0 - beta_second**STEP
    update = (
        moment_one_new / correct_one / (jnp.sqrt(moment_two_new / correct_two) + epsilon)
        + weight_decay * weights
    )
    return (moment_one_new, moment_two_new, weights - learn_rate * update)


def shards(inputs, value_cotangent, master, first_moment, second_moment):
    fsdp = tuple(a for a in ("y", "xh", "c"))
    sizes = tuple(lax.axis_size(a) for a in ("zh", "zl", "xl"))
    rows, _, slice_width = master.shape
    core = lax.axis_index("c").astype(jnp.int32).reshape(1)
    outgoing = partials("send", sizes, rows, core, inputs, value_cotangent)
    arrived = lax.ppermute(outgoing, "c", [(0, 1), (1, 0)])
    kept = partials("keep", sizes, rows, core, inputs, value_cotangent)
    chip_sum = (kept + arrived.astype(jnp.float32)).astype(jnp.bfloat16)
    parts = lax.all_to_all(chip_sum, ("zl", "xl"), 0, 0, tiled=True)
    blocks = regroup(parts, sizes[0])
    peers = sizes[0] * lax.axis_size("y") * lax.axis_size("xh")
    terms = lax.all_to_all(blocks.reshape(peers, 2, -1), ("zh", "y", "xh"), 0, 0, tiled=True)
    gradient = jnp.sum(terms.astype(jnp.float32), axis=0).reshape(rows, KVH, slice_width)
    moment_one_new, moment_two_new, master_new = adam_update(
        gradient, first_moment, second_moment, master
    )
    by_head = jnp.transpose(master_new.astype(jnp.bfloat16), (1, 0, 2))
    devices = math.prod(lax.axis_size(a) for a in fsdp)
    outgoing = jnp.tile(by_head, (devices // KVH, 1, 1))
    arrived = lax.all_to_all(outgoing, fsdp, 0, 0, tiled=True)
    return (moment_one_new, moment_two_new, master_new, arrived.reshape(1, -1, slice_width))


def solution(mesh):
    grid = mesh.devices.reshape(8, 4, 2, 4, 2, 2)
    fine = Mesh(grid, ("y", "xh", "c", "zh", "zl", "xl"))
    fsdp, dp = ("y", "xh", "c"), ("zh", "zl", "xl")
    tokens = P(fsdp + dp, None)
    owned = P(fsdp, None, dp)
    return jax.shard_map(
        shards,
        mesh=fine,
        in_specs=(tokens, tokens, owned, owned, owned),
        out_specs=(owned, owned, owned, owned),
        check_vma=False,
    )
```

time: 135 us -> 106 us (0.79)
  blocking collectives: 123 us -> 73.3 us
  starting transfers between devices: 0 us -> 16 us
  Pallas kernels: 0 us -> 10.3 us
  local copies, waits for them, and re-layouts: 5.54 us -> 2.5 us
  matrix products: 1.83 us -> 0 us
    all_to_all x3, blocking collectives: 123 us -> 73.3 us  [the longest x1 33.3 us: shards(): lax.all_to_all(blocks.reshape(peers, 2, -1), ('zh', 'y', 'xh'), 0, 0, til...]
    ppermute x0 -> x1, starting transfers between devices: none -> 16 us  [shards(): arrived = lax.ppermute(outgoing, 'c', [(0, 1), (1, 0)])]
    pallas_call x0 -> x3, Pallas kernels: none -> 10.3 us  [the longest x2 7.79 us: partials(): pl.pallas_call(lambda *refs: partial_kernel(sizes, rows, which, *refs), o...]
    unnamed x12 -> x8, local copies, waits for them, and re-layouts: 3.18 us -> 0.3 us
    convert_element_type x0 -> x1, other arithmetic: none -> 2 us  [shards(): chip_sum = (kept + arrived.astype(jnp.float32)).astype(jnp.bfloat16)]
    reduce_sum x2 -> x1, other arithmetic: 2.27 us -> 0.32 us  [shards(): jnp.sum(terms.astype(jnp.float32), axis=0).reshape(rows, KVH, slice_width)]
    dot_general x1 -> x0, matrix products: 1.83 us -> none  [shards(): lax.dot_general(inputs, value_cotangent, (((0,), (0,)), ((), ())), prefer...]
  transfers between devices with their start and end apart: 0 -> 1, of which waited for: 0 -> 0; matrix products, arithmetic and copies ran while one was open for 0% -> 0% of each run, Pallas kernels for 0% -> 4%
where the time goes in v2:
time: 106 us
  blocking collectives  73.3 us (69%)
  starting transfers between devices  16 us (15%)
  Pallas kernels  10.3 us (10%)
  other arithmetic  2.96 us (3%)
  local copies, waits for them, and re-layouts  2.5 us (2%)
    all_to_all x1, blocking collectives, shards(): lax.all_to_all(blocks.reshape(peers, 2, -1), ('zh', 'y', 'xh'), 0, 0, til...  33.3 us
    all_to_all x1, blocking collectives, shards(): arrived = lax.all_to_all(outgoing, fsdp, 0, 0, tiled=True)  20.3 us
    all_to_all x1, blocking collectives, shards(): parts = lax.all_to_all(chip_sum, ('zl', 'xl'), 0, 0, tiled=True)  19.6 us
    ppermute x1, starting transfers between devices, shards(): arrived = lax.ppermute(outgoing, 'c', [(0, 1), (1, 0)])  16 us
    pallas_call x2, Pallas kernels, partials(): pl.pallas_call(lambda *refs: partial_kernel(sizes, rows, which, *refs), o...  7.79 us
    pallas_call x1, Pallas kernels, regroup(): pl.pallas_call(lambda *refs: regroup_kernel(z_hi, *refs), out_shape=jax.S...  2.54 us
  transfers between devices with their start and end apart: 1, of which 0 were waited for; matrix products, arithmetic and copies ran while one was open for 0% of the time, Pallas kernels for 4%

profile of v2, /device:TPU:1, one launch (start us, length us, event | category | flops | bytes accessed | tf_op | source)
XLA Modules:
  0.0 105.8 jit_solution(12722856373999988735)
XLA Ops:
  0.6 3.7 %partial_send.1 = bf16[4,1280,128]{2,1,0:T(8,128)(2,1)} custom-call(s32[1]{0:T(128)} %bitcast.refs_0_, bf16[256,2560]{1,0:T(8,128)(2,1)} %refs_1_.3, bf16[256,512]{1,0:T(8,128)(2,1)} %refs_2_.3), custom_call_target="tpu_custom_call" | custom-call | flops 671088640 | bytes 3145728 | tf_op jit(solution)/shard_map/partial_send/pallas_call | solution.py:71
  4.3 16.0 %collective-permute-start = (bf16[4,1280,128]{2,1,0:T(8,128)(2,1)}, bf16[4,1280,128]{2,1,0:T(8,128)(2,1)S(1)}, u32[]{:S(2)}, u32[]{:S(2)}) collective-permute-start(bf16[4,1280,128]{2,1,0:T(8,128)(2,1)} %partial_send.1), channel_id=1, source_target_pairs={{0,16},{16,0},{1,17},{17,1},{2,18},{18,2},{3,19},{19,3},{4,20},{20... | collective-permute-start | bytes 3932168 | tf_op jit(solution)/shard_map/ppermute | solution.py:130
  20.3 4.1 %partial_keep.1 = f32[4,1280,128]{2,1,0:T(8,128)} custom-call(s32[1]{0:T(128)} %bitcast.refs_0_, bf16[256,2560]{1,0:T(8,128)(2,1)} %refs_1_.3, bf16[256,512]{1,0:T(8,128)(2,1)} %refs_2_.3), custom_call_target="tpu_custom_call" | custom-call | flops 671088640 | bytes 3145728 | tf_op jit(solution)/shard_map/partial_keep/pallas_call | solution.py:71
  24.4 0.0 collective-permute-done
  24.4 2.0 %add_convert_fusion = bf16[4,1280,128]{2,1,0:T(8,128)(2,1)S(1)} fusion(f32[4,1280,128]{2,1,0:T(8,128)} %partial_keep.1, bf16[4,1280,128]{2,1,0:T(8,128)(2,1)S(1)} %collective-permute-done), kind=kLoop, calls=%fused_computation | loop fusion | flops 1966080 | bytes 5242880 | tf_op jit(solution)/shard_map/convert_element_type | solution.py:132
  26.4 19.6 %all_to_all.15.refs_0_ = bf16[4,1280,128]{2,1,0:T(8,128)(2,1)} all-to-all(bf16[4,1280,128]{2,1,0:T(8,128)(2,1)S(1)} %add_convert_fusion), channel_id=1, replica_groups=mesh['y'=8,'xh'=4,'c'=2,'zh'=4,'zl'=2,'xl'=2] {'zl','xl'}, dimensions={0} | all-to-all | bytes 2621440 | tf_op jit(solution)/shard_map/all_to_all | solution.py:133
  46.1 2.5 %regroup.1 = bf16[4,320,128]{2,1,0:T(8,128)(2,1)} custom-call(bf16[4,1280,128]{2,1,0:T(8,128)(2,1)} %all_to_all.15.refs_0_), custom_call_target="tpu_custom_call" | custom-call | tf_op jit(solution)/shard_map/regroup/pallas_call | solution.py:102
  48.6 0.0 copy-start
  48.6 0.0 copy-start.1
  48.6 0.0 copy-start.2
  48.6 1.1 %reshape.25 = bf16[128,2,640]{2,1,0:T(2,128)(2,1)S(1)} reshape(bf16[4,320,128]{2,1,0:T(8,128)(2,1)} %regroup.1) | data formatting | bytes 655360 | tf_op jit(solution)/shard_map/reshape | solution.py:136
  49.8 33.3 %all_to_all.16 = bf16[128,2,640]{2,1,0:T(2,128)(2,1)S(1)} all-to-all(bf16[128,2,640]{2,1,0:T(2,128)(2,1)S(1)} %reshape.25), channel_id=1, replica_groups=mesh['y'=8,'xh'=4,'c'=2,'zh'=4,'zl'=2,'xl'=2] {'zh','y','xh'}, dimensions={0} | all-to-all | bytes 655360 | tf_op jit(solution)/shard_map/all_to_all | solution.py:136
  83.1 0.3 convert_reduce_fusion
  83.4 0.1 reshape.26
  83.6 0.1 copy.33
  83.6 0.0 copy-done
  83.7 0.0 copy-done.1
  83.7 0.0 copy-done.2
  83.7 0.6 convert_bitcast_fusion
  84.3 0.2 reshape.28
  84.5 20.3 %all_to_all.17 = bf16[64,2,160]{2,1,0:T(2,128)(2,1)S(1)} all-to-all(bf16[64,2,160]{2,1,0:T(2,128)(2,1)S(1)} %reshape.28), channel_id=1, replica_groups=mesh['y'=8,'xh'=4,'c'=2,'zh'=4,'zl'=2,'xl'=2] {'y','xh','c'}, dimensions={0} | all-to-all | bytes 81920 | tf_op jit(solution)/shard_map/all_to_all | solution.py:144
  104.8 0.1 reshape.29
  105.0 0.8 reshape.27
  (2 shorter events, 0.0 us)
Async XLA Ops:
  4.3 20.1 %collective-permute-start = (bf16[4,1280,128]{2,1,0:T(8,128)(2,1)}, bf16[4,1280,128]{2,1,0:T(8,128)(2,1)S(1)}, u32[]{:S(2)}, u32[]{:S(2)}) collective-permute-start(bf16[4,1280,128]{2,1,0:T(8,128)(2,1)} %partial_send.1), channel_id=1, source_target_pairs={{0,16},{16,0},{1,17},{17,1},{2,18},{18,2},{3,19},{19,3},{4,20},{20... | collective-permute-start | bytes 3932168 | tf_op jit(solution)/shard_map/ppermute | solution.py:130
  48.6 35.0 %copy-start = (f32[40,4,8]{0,2,1:T(8,128)S(1)}, f32[40,4,8]{0,2,1:T(8,128)}, u32[]{:S(2)}) copy-start(f32[40,4,8]{0,2,1:T(8,128)} %param.7) | copy-start | bytes 15364
  48.6 35.0 %copy-start.1 = (f32[40,4,8]{0,2,1:T(8,128)S(1)}, f32[40,4,8]{0,2,1:T(8,128)}, u32[]{:S(2)}) copy-start(f32[40,4,8]{0,2,1:T(8,128)} %param.9) | copy-start | bytes 15364
  48.6 35.0 %copy-start.2 = (f32[40,4,8]{0,2,1:T(8,128)S(1)}, f32[40,4,8]{0,2,1:T(8,128)}, u32[]{:S(2)}) copy-start(f32[40,4,8]{0,2,1:T(8,128)} %param.8) | copy-start | bytes 15364

commit v3 on v2

--- a/solution.py
+++ b/solution.py
@@ -46,11 +46,11 @@
     order = column_order(z_hi, z_lo, x_lo)
     cot = jnp.dot(cot_ref[...], order, preferred_element_type=jnp.float32).astype(jnp.bfloat16)
     parity = core_ref[0] if which == "keep" else 1 - core_ref[0]
-    d_in = x_ref.shape[1]
-    chunk = 640
+    chunk = acc.shape[1]
     pairs = chunk // (2 * rows)
-    for c in range(d_in // chunk):
-        acc[...] = lax.dot_general(
+    for c in range(x_ref.shape[1] // chunk):
+        slot = c % acc.shape[0]
+        acc[slot] = lax.dot_general(
             x_ref[:, c * chunk : (c + 1) * chunk],
             cot,
             (((0,), (0,)), ((), ())),
@@ -58,14 +58,14 @@
         )
         for k in range(pairs):
             start = pl.multiple_of((2 * k + parity) * rows, 8)
-            block = acc[pl.ds(start, rows), :]
+            block = acc[slot, pl.ds(start, rows), :]
             at = (c * pairs + k) * rows
             for b in range(z_lo * x_lo):
                 out_ref[b, at : at + rows, :] = block[:, b * LANES : (b + 1) * LANES].astype(out_ref.dtype)
 
 
 def partials(which, sizes, rows, core, x, cot):
-    d_in = x.shape[1]
+    tokens, d_in = x.shape
     blocks = sizes[1] * sizes[2]
     dtype = jnp.float32 if which == "keep" else jnp.bfloat16
     return pl.pallas_call(
@@ -73,8 +73,9 @@
         out_shape=jax.ShapeDtypeStruct((blocks, d_in // 2, LANES), dtype),
         in_specs=[SMEM, VMEM, VMEM],
         out_specs=VMEM,
-        scratch_shapes=[pltpu.VMEM((640, KVH * HEAD), jnp.float32)],
-        cost_estimate=pl.CostEstimate(flops=2 * x.shape[0] * d_in * KVH * HEAD, bytes_accessed=3 << 20, transcendentals=0),
+        scratch_shapes=[pltpu.VMEM((2, 640, KVH * HEAD), jnp.float32)],
+        cost_estimate=pl.CostEstimate(flops=2 * tokens * d_in * KVH * HEAD, bytes_accessed=3 << 20, transcendentals=0),
+        compiler_params=pltpu.CompilerParams(vmem_limit_bytes=16 << 20),
         name="partial_" + which,
     )(core, x, cot)
 
@@ -94,17 +95,18 @@
             shift = (q - zh) * width % LANES
             moved = quarters[q] if shift == 0 else pltpu.roll(quarters[q], shift, 1)
             out = jnp.where(lane == q, moved, out)
-        out_ref[zh] = out.astype(out_ref.dtype)
+        out_ref[zh * n : (zh + 1) * n, :] = out.astype(out_ref.dtype)
 
 
 def regroup(parts, z_hi):
     rows = parts.shape[1]
     return pl.pallas_call(
         lambda *refs: regroup_kernel(z_hi, *refs),
-        out_shape=jax.ShapeDtypeStruct((z_hi, rows // z_hi, LANES), jnp.bfloat16),
+        out_shape=jax.ShapeDtypeStruct((rows, LANES), jnp.bfloat16),
         in_specs=[VMEM],
         out_specs=VMEM,
         scratch_shapes=[pltpu.VMEM((rows, LANES), jnp.float32)],
+        compiler_params=pltpu.CompilerParams(vmem_limit_bytes=16 << 20),
         name="regroup",
     )(parts)
 
@@ -133,8 +135,9 @@
     parts = lax.all_to_all(chip_sum, ("zl", "xl"), 0, 0, tiled=True)
     blocks = regroup(parts, sizes[0])
     peers = sizes[0] * lax.axis_size("y") * lax.axis_size("xh")
-    terms = lax.all_to_all(blocks.reshape(peers, 2, -1), ("zh", "y", "xh"), 0, 0, tiled=True)
-    gradient = jnp.sum(terms.astype(jnp.float32), axis=0).reshape(rows, KVH, slice_width)
+    terms = lax.all_to_all(blocks.reshape(-1, 2, LANES), ("zh", "y", "xh"), 0, 0, tiled=True)
+    terms = terms.reshape(peers, -1, 2, LANES).astype(jnp.float32)
+    gradient = jnp.sum(terms, axis=0).reshape(rows, KVH, slice_width)
     moment_one_new, moment_two_new, master_new = adam_update(
         gradient, first_moment, second_moment, master
     )

time: 106 us -> 98 us (0.925)
  Pallas kernels: 10.3 us -> 3.06 us
  other arithmetic: 2.96 us -> 1.22 us
  blocking collectives: 73.3 us -> 71.7 us
  waiting for transfers between devices: 0.01 us -> 1.33 us
  local copies, waits for them, and re-layouts: 2.5 us -> 3.63 us
    pallas_call x2, Pallas kernels: 7.79 us -> 2.56 us  [partials(): pl.pallas_call(lambda *refs: partial_kernel(sizes, rows, which, *refs), o...]
    unnamed x8 -> x12, local copies, waits for them, and re-layouts: 0.3 us -> 2.56 us
    pallas_call x1, Pallas kernels: 2.54 us -> 0.5 us  [regroup(): pl.pallas_call(lambda *refs: regroup_kernel(z_hi, *refs), out_shape=jax.S...]
    convert_element_type x1, other arithmetic: 2 us -> 0.26 us  [shards(): chip_sum = (kept + arrived.astype(jnp.float32)).astype(jnp.bfloat16)]
    all_to_all x1, blocking collectives: 20.3 us -> 18.7 us  [shards(): arrived = lax.all_to_all(outgoing, fsdp, 0, 0, tiled=True)]
    ppermute x1, waiting for transfers between devices: 0.01 us -> 1.33 us  [shards(): arrived = lax.ppermute(outgoing, 'c', [(0, 1), (1, 0)])]
    reshape x3 -> x2, local copies, waits for them, and re-layouts: 1.36 us -> 0.22 us  [shards(): gradient = jnp.sum(terms, axis=0).reshape(rows, KVH, slice_width)]
  transfers between devices with their start and end apart: 1 -> 1, of which waited for: 0 -> 1; matrix products, arithmetic and copies ran while one was open for 0% -> 0% of each run, Pallas kernels for 4% -> 1%
where the time goes in v3:
time: 98 us; the launch traced here: 97.7 us
  blocking collectives  71.7 us (73%)
  starting transfers between devices  16 us (16%)
  local copies, waits for them, and re-layouts  3.63 us (4%)
  Pallas kernels  3.06 us (3%)
  waiting for transfers between devices  1.33 us (1%)
  other arithmetic  1.22 us (1%)
    all_to_all x1, blocking collectives, shards(): lax.all_to_all(blocks.reshape(-1, 2, LANES), ('zh', 'y', 'xh'), 0, 0, til...  34.3 us
    all_to_all x1, blocking collectives, shards(): parts = lax.all_to_all(chip_sum, ('zl', 'xl'), 0, 0, tiled=True)  18.8 us
    all_to_all x1, blocking collectives, shards(): arrived = lax.all_to_all(outgoing, fsdp, 0, 0, tiled=True)  18.7 us
    ppermute x1, starting transfers between devices, shards(): arrived = lax.ppermute(outgoing, 'c', [(0, 1), (1, 0)])  16 us
    unnamed x12, local copies, waits for them, and re-layouts  2.56 us
    pallas_call x2, Pallas kernels, partials(): pl.pallas_call(lambda *refs: partial_kernel(sizes, rows, which, *refs), o...  2.56 us
  transfers between devices with their start and end apart: 1, of which 1 were waited for; matrix products, arithmetic and copies ran while one was open for 0% of the time, Pallas kernels for 1%

profile of v3, /device:TPU:1, one launch (start us, length us, event | category | flops | bytes accessed | tf_op | source)
XLA Modules:
  0.0 97.7 jit_solution(17217528259381990753)
XLA Ops:
  0.6 0.0 copy-start
  0.6 1.3 %copy-done = bf16[256,2560]{1,0:T(8,128)(2,1)S(1)} copy-done((bf16[256,2560]{1,0:T(8,128)(2,1)S(1)}, bf16[256,2560]{1,0:T(8,128)(2,1)}, u32[]{:S(2)}) %copy-start) | copy-done | bytes 1310744
  2.0 0.0 copy-start.1
  2.0 0.9 copy-done.1
  2.9 1.3 %partial_send.1 = bf16[4,1280,128]{2,1,0:T(8,128)(2,1)S(1)} custom-call(s32[1]{0:T(128)} %bitcast.refs_0_, bf16[256,2560]{1,0:T(8,128)(2,1)S(1)} %copy-done, bf16[256,512]{1,0:T(8,128)(2,1)S(1)} %copy-done.1), custom_call_target="tpu_custom_call" | custom-call | flops 671088640 | bytes 3145728 | tf_op jit(solution)/shard_map/partial_send/pallas_call | solution.py:71
  4.2 16.0 %collective-permute-start = (bf16[4,1280,128]{2,1,0:T(8,128)(2,1)S(1)}, bf16[4,1280,128]{2,1,0:T(8,128)(2,1)S(1)}, u32[]{:S(2)}, u32[]{:S(2)}) collective-permute-start(bf16[4,1280,128]{2,1,0:T(8,128)(2,1)S(1)} %partial_send.1), channel_id=1, source_target_pairs={{0,16},{16,0},{1,17},{17,1},{2,18},{18,2},{3,19},{19,3},{4,20},{20... | collective-permute-start | bytes 3932168 | tf_op jit(solution)/shard_map/ppermute | solution.py:132
  20.2 1.3 %partial_keep.1 = f32[4,1280,128]{2,1,0:T(8,128)S(1)} custom-call(s32[1]{0:T(128)} %bitcast.refs_0_, bf16[256,2560]{1,0:T(8,128)(2,1)S(1)} %copy-done, bf16[256,512]{1,0:T(8,128)(2,1)S(1)} %copy-done.1), custom_call_target="tpu_custom_call" | custom-call | flops 671088640 | bytes 3145728 | tf_op jit(solution)/shard_map/partial_keep/pallas_call | solution.py:71
  21.5 1.3 %collective-permute-done = bf16[4,1280,128]{2,1,0:T(8,128)(2,1)S(1)} collective-permute-done((bf16[4,1280,128]{2,1,0:T(8,128)(2,1)S(1)}, bf16[4,1280,128]{2,1,0:T(8,128)(2,1)S(1)}, u32[]{:S(2)}, u32[]{:S(2)}) %collective-permute-start) | collective-permute-done | bytes 1310752 | tf_op jit(solution)/shard_map/ppermute | solution.py:132
  22.8 0.3 add_convert_fusion
  23.1 18.8 %all_to_all.15.refs_0_ = bf16[4,1280,128]{2,1,0:T(8,128)(2,1)S(1)} all-to-all(bf16[4,1280,128]{2,1,0:T(8,128)(2,1)S(1)} %add_convert_fusion), channel_id=1, replica_groups=mesh['y'=8,'xh'=4,'c'=2,'zh'=4,'zl'=2,'xl'=2] {'zl','xl'}, dimensions={0} | all-to-all | bytes 2621440 | tf_op jit(solution)/shard_map/all_to_all | solution.py:135
  41.9 0.0 copy-start.2
  41.9 0.0 copy-start.3
  41.9 0.0 copy-start.4
  41.9 0.5 regroup.1
  42.4 34.3 %all_to_all.16 = bf16[640,2,128]{2,1,0:T(2,128)(2,1)S(1)} all-to-all(bf16[640,2,128]{2,1,0:T(2,128)(2,1)S(1)} %bitcast.11), channel_id=1, replica_groups=mesh['y'=8,'xh'=4,'c'=2,'zh'=4,'zl'=2,'xl'=2] {'zh','y','xh'}, dimensions={0} | all-to-all | bytes 655360 | tf_op jit(solution)/shard_map/all_to_all | solution.py:138
  76.6 0.3 convert_reduce_fusion
  76.9 0.1 reshape.29
  77.1 0.1 copy.33
  77.2 0.0 copy-done.2
  77.2 0.0 copy-done.3
  77.2 0.0 copy-done.4
  77.2 0.6 convert_bitcast_fusion
  77.9 0.2 reshape.32
  78.0 18.7 %all_to_all.17 = bf16[64,2,160]{2,1,0:T(2,128)(2,1)S(1)} all-to-all(bf16[64,2,160]{2,1,0:T(2,128)(2,1)S(1)} %reshape.32), channel_id=1, replica_groups=mesh['y'=8,'xh'=4,'c'=2,'zh'=4,'zl'=2,'xl'=2] {'y','xh','c'}, dimensions={0} | all-to-all | bytes 81920 | tf_op jit(solution)/shard_map/all_to_all | solution.py:147
  96.7 0.1 reshape.33
  96.8 0.8 reshape.30
  (2 shorter events, 0.0 us)
Async XLA Ops:
  0.6 1.3 %copy-start = (bf16[256,2560]{1,0:T(8,128)(2,1)S(1)}, bf16[256,2560]{1,0:T(8,128)(2,1)}, u32[]{:S(2)}) copy-start(bf16[256,2560]{1,0:T(8,128)(2,1)} %refs_1_.3) | copy-start | bytes 3932164
  2.0 0.9 copy-start.1
  4.2 18.7 %collective-permute-start = (bf16[4,1280,128]{2,1,0:T(8,128)(2,1)S(1)}, bf16[4,1280,128]{2,1,0:T(8,128)(2,1)S(1)}, u32[]{:S(2)}, u32[]{:S(2)}) collective-permute-start(bf16[4,1280,128]{2,1,0:T(8,128)(2,1)S(1)} %partial_send.1), channel_id=1, source_target_pairs={{0,16},{16,0},{1,17},{17,1},{2,18},{18,2},{3,19},{19,3},{4,20},{20... | collective-permute-start | bytes 3932168 | tf_op jit(solution)/shard_map/ppermute | solution.py:132
  41.9 35.3 %copy-start.2 = (f32[40,4,8]{0,2,1:T(8,128)S(1)}, f32[40,4,8]{0,2,1:T(8,128)}, u32[]{:S(2)}) copy-start(f32[40,4,8]{0,2,1:T(8,128)} %param.7) | copy-start | bytes 15364
  41.9 35.3 %copy-start.3 = (f32[40,4,8]{0,2,1:T(8,128)S(1)}, f32[40,4,8]{0,2,1:T(8,128)}, u32[]{:S(2)}) copy-start(f32[40,4,8]{0,2,1:T(8,128)} %param.9) | copy-start | bytes 15364
  41.9 35.3 %copy-start.4 = (f32[40,4,8]{0,2,1:T(8,128)S(1)}, f32[40,4,8]{0,2,1:T(8,128)}, u32[]{:S(2)}) copy-start(f32[40,4,8]{0,2,1:T(8,128)} %param.8) | copy-start | bytes 15364

commit v4 on v3

--- a/solution.py
+++ b/solution.py
@@ -41,20 +41,25 @@
     return one_hot(old == source).astype(jnp.bfloat16)
 
 
-def partial_kernel(sizes, rows, which, core_ref, x_ref, cot_ref, out_ref, acc):
+def partial_kernel(sizes, rows, which, core_ref, x_ref, cot_ref, out_ref, acc, held, held_cot, sems):
     z_hi, z_lo, x_lo = sizes
+    chunks, _, chunk = held.shape
+    copies = [pltpu.make_async_copy(cot_ref, held_cot, sems.at[chunks])]
+    copies += [
+        pltpu.make_async_copy(x_ref.at[:, pl.ds(c * chunk, chunk)], held.at[c], sems.at[c]) for c in range(chunks)
+    ]
+    for copy in copies:
+        copy.start()
     order = column_order(z_hi, z_lo, x_lo)
-    cot = jnp.dot(cot_ref[...], order, preferred_element_type=jnp.float32).astype(jnp.bfloat16)
+    copies[0].wait()
+    cot = jnp.dot(held_cot[...], order, preferred_element_type=jnp.float32).astype(jnp.bfloat16)
     parity = core_ref[0] if which == "keep" else 1 - core_ref[0]
-    chunk = acc.shape[1]
     pairs = chunk // (2 * rows)
-    for c in range(x_ref.shape[1] // chunk):
+    for c in range(chunks):
+        copies[c + 1].wait()
         slot = c % acc.shape[0]
         acc[slot] = lax.dot_general(
-            x_ref[:, c * chunk : (c + 1) * chunk],
-            cot,
-            (((0,), (0,)), ((), ())),
-            preferred_element_type=jnp.float32,
+            held[c], cot, (((0,), (0,)), ((), ())), preferred_element_type=jnp.float32
         )
         for k in range(pairs):
             start = pl.multiple_of((2 * k + parity) * rows, 8)
@@ -68,16 +73,23 @@
     tokens, d_in = x.shape
     blocks = sizes[1] * sizes[2]
     dtype = jnp.float32 if which == "keep" else jnp.bfloat16
+    chunk = 640
+    anywhere = pl.BlockSpec(memory_space=pl.ANY)
     return pl.pallas_call(
         lambda *refs: partial_kernel(sizes, rows, which, *refs),
         out_shape=jax.ShapeDtypeStruct((blocks, d_in // 2, LANES), dtype),
-        in_specs=[SMEM, VMEM, VMEM],
+        in_specs=[SMEM, anywhere, anywhere],
         out_specs=VMEM,
-        scratch_shapes=[pltpu.VMEM((2, 640, KVH * HEAD), jnp.float32)],
+        scratch_shapes=[
+            pltpu.VMEM((2, chunk, KVH * HEAD), jnp.float32),
+            pltpu.VMEM((d_in // chunk, tokens, chunk), jnp.bfloat16),
+            pltpu.VMEM(cot.shape, jnp.bfloat16),
+            pltpu.SemaphoreType.DMA((d_in // chunk + 1,)),
+        ],
         cost_estimate=pl.CostEstimate(flops=2 * tokens * d_in * KVH * HEAD, bytes_accessed=3 << 20, transcendentals=0),
         compiler_params=pltpu.CompilerParams(vmem_limit_bytes=16 << 20),
         name="partial_" + which,
-    )(core, x, cot)
+    )(core, *(pltpu.with_memory_space_constraint(a, pltpu.HBM) for a in (x, cot)))
 
 
 def regroup_kernel(z_hi, parts_ref, out_ref, acc):

time: 98 us -> 98.1 us (level)
  Pallas kernels: 3.06 us -> 6.23 us
  local copies, waits for them, and re-layouts: 3.63 us -> 1.37 us
  waiting for transfers between devices: 1.33 us -> 0.01 us
    pallas_call x2, Pallas kernels: 2.56 us -> 5.73 us  [partials(): pl.pallas_call(lambda *refs: partial_kernel(sizes, rows, which, *refs), o...]
    unnamed x12 -> x8, local copies, waits for them, and re-layouts: 2.56 us -> 0.3 us
    ppermute x1, waiting for transfers between devices: 1.33 us -> 0.01 us  [shards(): arrived = lax.ppermute(outgoing, 'c', [(0, 1), (1, 0)])]
  transfers between devices with their start and end apart: 1 -> 1, of which waited for: 1 -> 0; matrix products, arithmetic and copies ran while one was open for 0% -> 0% of each run, Pallas kernels for 1% -> 3%
where the time goes in v4:
time: 98.1 us; the launch traced here: 97.8 us
  blocking collectives  72.2 us (74%)
  starting transfers between devices  16 us (16%)
  Pallas kernels  6.23 us (6%)
  local copies, waits for them, and re-layouts  1.37 us (1%)
  other arithmetic  1.22 us (1%)
    all_to_all x1, blocking collectives, shards(): lax.all_to_all(blocks.reshape(-1, 2, LANES), ('zh', 'y', 'xh'), 0, 0, til...  34.1 us
    all_to_all x1, blocking collectives, shards(): arrived = lax.all_to_all(outgoing, fsdp, 0, 0, tiled=True)  19.3 us
    all_to_all x1, blocking collectives, shards(): parts = lax.all_to_all(chip_sum, ('zl', 'xl'), 0, 0, tiled=True)  18.8 us
    ppermute x1, starting transfers between devices, shards(): arrived = lax.ppermute(outgoing, 'c', [(0, 1), (1, 0)])  16 us
    pallas_call x2, Pallas kernels, partials(): pl.pallas_call(lambda *refs: partial_kernel(sizes, rows, which, *refs), o...  5.73 us
  transfers between devices with their start and end apart: 1, of which 0 were waited for; matrix products, arithmetic and copies ran while one was open for 0% of the time, Pallas kernels for 3%

profile of v4, /device:TPU:1, one launch (start us, length us, event | category | flops | bytes accessed | tf_op | source)
XLA Modules:
  0.0 97.8 jit_solution(3024349561523945733)
XLA Ops:
  0.6 2.9 %partial_send.1 = bf16[4,1280,128]{2,1,0:T(8,128)(2,1)S(1)} custom-call(s32[1]{0:T(128)} %bitcast.refs_0_, bf16[256,2560]{1,0:T(8,128)(2,1)} %refs_1_.3, bf16[256,512]{1,0:T(8,128)(2,1)} %refs_2_.3), custom_call_target="tpu_custom_call" | custom-call | flops 671088640 | bytes 3145728 | tf_op jit(solution)/shard_map/partial_send/pallas_call | solution.py:78
  3.5 16.0 %collective-permute-start = (bf16[4,1280,128]{2,1,0:T(8,128)(2,1)S(1)}, bf16[4,1280,128]{2,1,0:T(8,128)(2,1)S(1)}, u32[]{:S(2)}, u32[]{:S(2)}) collective-permute-start(bf16[4,1280,128]{2,1,0:T(8,128)(2,1)S(1)} %partial_send.1), channel_id=1, source_target_pairs={{0,16},{16,0},{1,17},{17,1},{2,18},{18,2},{3,19},{19,3},{4,20},{20... | collective-permute-start | bytes 3932168 | tf_op jit(solution)/shard_map/ppermute | solution.py:144
  19.5 2.9 %partial_keep.1 = f32[4,1280,128]{2,1,0:T(8,128)S(1)} custom-call(s32[1]{0:T(128)} %bitcast.refs_0_, bf16[256,2560]{1,0:T(8,128)(2,1)} %refs_1_.3, bf16[256,512]{1,0:T(8,128)(2,1)} %refs_2_.3), custom_call_target="tpu_custom_call" | custom-call | flops 671088640 | bytes 3145728 | tf_op jit(solution)/shard_map/partial_keep/pallas_call | solution.py:78
  22.4 0.0 collective-permute-done
  22.4 0.3 add_convert_fusion
  22.7 18.8 %all_to_all.15.refs_0_ = bf16[4,1280,128]{2,1,0:T(8,128)(2,1)S(1)} all-to-all(bf16[4,1280,128]{2,1,0:T(8,128)(2,1)S(1)} %add_convert_fusion), channel_id=1, replica_groups=mesh['y'=8,'xh'=4,'c'=2,'zh'=4,'zl'=2,'xl'=2] {'zl','xl'}, dimensions={0} | all-to-all | bytes 2621440 | tf_op jit(solution)/shard_map/all_to_all | solution.py:147
  41.5 0.0 copy-start
  41.5 0.0 copy-start.1
  41.5 0.0 copy-start.2
  41.5 0.5 regroup.1
  42.0 34.1 %all_to_all.16 = bf16[640,2,128]{2,1,0:T(2,128)(2,1)S(1)} all-to-all(bf16[640,2,128]{2,1,0:T(2,128)(2,1)S(1)} %bitcast.11), channel_id=1, replica_groups=mesh['y'=8,'xh'=4,'c'=2,'zh'=4,'zl'=2,'xl'=2] {'zh','y','xh'}, dimensions={0} | all-to-all | bytes 655360 | tf_op jit(solution)/shard_map/all_to_all | solution.py:150
  76.1 0.3 convert_reduce_fusion
  76.4 0.1 reshape.29
  76.5 0.1 copy.33
  76.6 0.0 copy-done
  76.6 0.0 copy-done.1
  76.6 0.0 copy-done.2
  76.6 0.6 convert_bitcast_fusion
  77.3 0.2 reshape.32
  77.5 19.3 %all_to_all.17 = bf16[64,2,160]{2,1,0:T(2,128)(2,1)S(1)} all-to-all(bf16[64,2,160]{2,1,0:T(2,128)(2,1)S(1)} %reshape.32), channel_id=1, replica_groups=mesh['y'=8,'xh'=4,'c'=2,'zh'=4,'zl'=2,'xl'=2] {'y','xh','c'}, dimensions={0} | all-to-all | bytes 81920 | tf_op jit(solution)/shard_map/all_to_all | solution.py:159
  96.8 0.1 reshape.33
  96.9 0.8 reshape.30
  (2 shorter events, 0.0 us)
Async XLA Ops:
  3.5 18.9 %collective-permute-start = (bf16[4,1280,128]{2,1,0:T(8,128)(2,1)S(1)}, bf16[4,1280,128]{2,1,0:T(8,128)(2,1)S(1)}, u32[]{:S(2)}, u32[]{:S(2)}) collective-permute-start(bf16[4,1280,128]{2,1,0:T(8,128)(2,1)S(1)} %partial_send.1), channel_id=1, source_target_pairs={{0,16},{16,0},{1,17},{17,1},{2,18},{18,2},{3,19},{19,3},{4,20},{20... | collective-permute-start | bytes 3932168 | tf_op jit(solution)/shard_map/ppermute | solution.py:144
  41.5 35.1 %copy-start = (f32[40,4,8]{0,2,1:T(8,128)S(1)}, f32[40,4,8]{0,2,1:T(8,128)}, u32[]{:S(2)}) copy-start(f32[40,4,8]{0,2,1:T(8,128)} %param.7) | copy-start | bytes 15364
  41.5 35.1 %copy-start.1 = (f32[40,4,8]{0,2,1:T(8,128)S(1)}, f32[40,4,8]{0,2,1:T(8,128)}, u32[]{:S(2)}) copy-start(f32[40,4,8]{0,2,1:T(8,128)} %param.9) | copy-start | bytes 15364
  41.5 35.1 %copy-start.2 = (f32[40,4,8]{0,2,1:T(8,128)S(1)}, f32[40,4,8]{0,2,1:T(8,128)}, u32[]{:S(2)}) copy-start(f32[40,4,8]{0,2,1:T(8,128)} %param.8) | copy-start | bytes 15364

commit v5 on v4

--- a/solution.py
+++ b/solution.py
@@ -42,7 +42,7 @@
 
 
 def partial_kernel(sizes, rows, which, core_ref, x_ref, cot_ref, out_ref, acc, held, held_cot, sems):
-    z_hi, z_lo, x_lo = sizes
+    z_hi, z_lo, x_lo, y_lo, x_hi = sizes
     chunks, _, chunk = held.shape
     copies = [pltpu.make_async_copy(cot_ref, held_cot, sems.at[chunks])]
     copies += [
@@ -55,6 +55,7 @@
     cot = jnp.dot(held_cot[...], order, preferred_element_type=jnp.float32).astype(jnp.bfloat16)
     parity = core_ref[0] if which == "keep" else 1 - core_ref[0]
     pairs = chunk // (2 * rows)
+    span = x_hi * rows
     for c in range(chunks):
         copies[c + 1].wait()
         slot = c % acc.shape[0]
@@ -64,20 +65,21 @@
         for k in range(pairs):
             start = pl.multiple_of((2 * k + parity) * rows, 8)
             block = acc[slot, pl.ds(start, rows), :]
-            at = (c * pairs + k) * rows
+            y, x = divmod(c * pairs + k, x_hi)
+            at = y // y_lo * span + x * rows
             for b in range(z_lo * x_lo):
-                out_ref[b, at : at + rows, :] = block[:, b * LANES : (b + 1) * LANES].astype(out_ref.dtype)
+                out_ref[y % y_lo * z_lo * x_lo + b, at : at + rows, :] = block[:, b * LANES : (b + 1) * LANES].astype(out_ref.dtype)
 
 
 def partials(which, sizes, rows, core, x, cot):
     tokens, d_in = x.shape
-    blocks = sizes[1] * sizes[2]
+    blocks = math.prod(sizes[1:4])
     dtype = jnp.float32 if which == "keep" else jnp.bfloat16
     chunk = 640
     anywhere = pl.BlockSpec(memory_space=pl.ANY)
     return pl.pallas_call(
         lambda *refs: partial_kernel(sizes, rows, which, *refs),
-        out_shape=jax.ShapeDtypeStruct((blocks, d_in // 2, LANES), dtype),
+        out_shape=jax.ShapeDtypeStruct((blocks, 2 * d_in // blocks, LANES), dtype),
         in_specs=[SMEM, anywhere, anywhere],
         out_specs=VMEM,
         scratch_shapes=[
@@ -136,18 +138,18 @@
 
 
 def shards(inputs, value_cotangent, master, first_moment, second_moment):
-    fsdp = tuple(a for a in ("y", "xh", "c"))
-    sizes = tuple(lax.axis_size(a) for a in ("zh", "zl", "xl"))
+    fsdp = ("yh", "yl", "xh", "c")
+    sizes = tuple(lax.axis_size(a) for a in ("zh", "zl", "xl", "yl", "xh"))
     rows, _, slice_width = master.shape
     core = lax.axis_index("c").astype(jnp.int32).reshape(1)
     outgoing = partials("send", sizes, rows, core, inputs, value_cotangent)
     arrived = lax.ppermute(outgoing, "c", [(0, 1), (1, 0)])
     kept = partials("keep", sizes, rows, core, inputs, value_cotangent)
     chip_sum = (kept + arrived.astype(jnp.float32)).astype(jnp.bfloat16)
-    parts = lax.all_to_all(chip_sum, ("zl", "xl"), 0, 0, tiled=True)
+    parts = lax.all_to_all(chip_sum, ("yl", "zl", "xl"), 0, 0, tiled=True)
     blocks = regroup(parts, sizes[0])
-    peers = sizes[0] * lax.axis_size("y") * lax.axis_size("xh")
-    terms = lax.all_to_all(blocks.reshape(-1, 2, LANES), ("zh", "y", "xh"), 0, 0, tiled=True)
+    peers = sizes[0] * lax.axis_size("yh") * lax.axis_size("xh")
+    terms = lax.all_to_all(blocks.reshape(-1, 2, LANES), ("zh", "yh", "xh"), 0, 0, tiled=True)
     terms = terms.reshape(peers, -1, 2, LANES).astype(jnp.float32)
     gradient = jnp.sum(terms, axis=0).reshape(rows, KVH, slice_width)
     moment_one_new, moment_two_new, master_new = adam_update(
@@ -161,9 +163,9 @@
 
 
 def solution(mesh):
-    grid = mesh.devices.reshape(8, 4, 2, 4, 2, 2)
-    fine = Mesh(grid, ("y", "xh", "c", "zh", "zl", "xl"))
-    fsdp, dp = ("y", "xh", "c"), ("zh", "zl", "xl")
+    grid = mesh.devices.reshape(4, 2, 4, 2, 4, 2, 2)
+    fine = Mesh(grid, ("yh", "yl", "xh", "c", "zh", "zl", "xl"))
+    fsdp, dp = ("yh", "yl", "xh", "c"), ("zh", "zl", "xl")
     tokens = P(fsdp + dp, None)
     owned = P(fsdp, None, dp)
     return jax.shard_map(

time: 98.1 us -> 95.5 us (0.973)
  blocking collectives: 72.2 us -> 69.9 us
    all_to_all x2, blocking collectives: 52.9 us -> 51.1 us  [the longest x1 30.8 us: shards(): lax.all_to_all(blocks.reshape(-1, 2, LANES), ('zh', 'yh', 'xh'), 0, 0, ti...]
where the time goes in v5:
time: 95.5 us; the launch traced here: 95.2 us
  blocking collectives  69.9 us (73%)
  starting transfers between devices  16 us (17%)
  Pallas kernels  6.1 us (6%)
  local copies, waits for them, and re-layouts  1.37 us (1%)
  other arithmetic  1.07 us (1%)
    all_to_all x1, blocking collectives, shards(): lax.all_to_all(blocks.reshape(-1, 2, LANES), ('zh', 'yh', 'xh'), 0, 0, ti...  30.8 us
    all_to_all x1, blocking collectives, shards(): parts = lax.all_to_all(chip_sum, ('yl', 'zl', 'xl'), 0, 0, tiled=True)  20.3 us
    all_to_all x1, blocking collectives, shards(): arrived = lax.all_to_all(outgoing, fsdp, 0, 0, tiled=True)  18.8 us
    ppermute x1, starting transfers between devices, shards(): arrived = lax.ppermute(outgoing, 'c', [(0, 1), (1, 0)])  16 us
    pallas_call x2, Pallas kernels, partials(): pl.pallas_call(lambda *refs: partial_kernel(sizes, rows, which, *refs), o...  5.73 us
  transfers between devices with their start and end apart: 1, of which 0 were waited for; matrix products, arithmetic and copies ran while one was open for 0% of the time, Pallas kernels for 3%

profile of v5, /device:TPU:1, one launch (start us, length us, event | category | flops | bytes accessed | tf_op | source)
XLA Modules:
  0.0 95.2 jit_solution(3911268714423227381)
XLA Ops:
  0.6 2.9 %partial_send.1 = bf16[8,640,128]{2,1,0:T(8,128)(2,1)S(1)} custom-call(s32[1]{0:T(128)} %bitcast.refs_0_, bf16[256,2560]{1,0:T(8,128)(2,1)} %refs_1_.3, bf16[256,512]{1,0:T(8,128)(2,1)} %refs_2_.3), custom_call_target="tpu_custom_call" | custom-call | flops 671088640 | bytes 3145728 | tf_op jit(solution)/shard_map/partial_send/pallas_call | solution.py:80
  3.5 16.0 %collective-permute-start = (bf16[8,640,128]{2,1,0:T(8,128)(2,1)S(1)}, bf16[8,640,128]{2,1,0:T(8,128)(2,1)S(1)}, u32[]{:S(2)}, u32[]{:S(2)}) collective-permute-start(bf16[8,640,128]{2,1,0:T(8,128)(2,1)S(1)} %partial_send.1), channel_id=1, source_target_pairs={{0,16},{16,0},{1,17},{17,1},{2,18},{18,2},{3,19},{19,3},{4,20},{20... | collective-permute-start | bytes 3932168 | tf_op jit(solution)/shard_map/ppermute | solution.py:146
  19.5 2.9 %partial_keep.1 = f32[8,640,128]{2,1,0:T(8,128)S(1)} custom-call(s32[1]{0:T(128)} %bitcast.refs_0_, bf16[256,2560]{1,0:T(8,128)(2,1)} %refs_1_.3, bf16[256,512]{1,0:T(8,128)(2,1)} %refs_2_.3), custom_call_target="tpu_custom_call" | custom-call | flops 671088640 | bytes 3145728 | tf_op jit(solution)/shard_map/partial_keep/pallas_call | solution.py:80
  22.4 0.0 collective-permute-done
  22.4 0.3 add_convert_fusion
  22.7 20.3 %all_to_all.15.refs_0_ = bf16[8,640,128]{2,1,0:T(8,128)(2,1)S(1)} all-to-all(bf16[8,640,128]{2,1,0:T(8,128)(2,1)S(1)} %add_convert_fusion), channel_id=1, replica_groups=mesh['yh'=4,'yl'=2,'xh'=4,'c'=2,'zh'=4,'zl'=2,'xl'=2] {'yl','zl','xl'}, dimensions={0} | all-to-all | bytes 2621440 | tf_op jit(solution)/shard_map/all_to_all | solution.py:149
  43.0 0.0 copy-start
  43.0 0.0 copy-start.1
  43.0 0.0 copy-start.2
  43.0 0.4 regroup.1
  43.4 30.8 %all_to_all.16 = bf16[320,2,128]{2,1,0:T(2,128)(2,1)S(1)} all-to-all(bf16[320,2,128]{2,1,0:T(2,128)(2,1)S(1)} %bitcast.11), channel_id=1, replica_groups=mesh['yh'=4,'yl'=2,'xh'=4,'c'=2,'zh'=4,'zl'=2,'xl'=2] {'zh','yh','xh'}, dimensions={0} | all-to-all | bytes 327680 | tf_op jit(solution)/shard_map/all_to_all | solution.py:152
  74.2 0.2 convert_reduce_fusion
  74.4 0.1 reshape.29
  74.5 0.1 copy.33
  74.6 0.0 copy-done
  74.6 0.0 copy-done.1
  74.6 0.0 copy-done.2
  74.6 0.6 convert_bitcast_fusion
  75.3 0.2 reshape.32
  75.4 18.8 %all_to_all.17 = bf16[64,2,160]{2,1,0:T(2,128)(2,1)S(1)} all-to-all(bf16[64,2,160]{2,1,0:T(2,128)(2,1)S(1)} %reshape.32), channel_id=1, replica_groups=mesh['yh'=4,'yl'=2,'xh'=4,'c'=2,'zh'=4,'zl'=2,'xl'=2] {'yh','yl','xh','c'}, dimensions={0} | all-to-all | bytes 81920 | tf_op jit(solution)/shard_map/all_to_all | solution.py:161
  94.2 0.1 reshape.33
  94.4 0.8 reshape.30
  (2 shorter events, 0.0 us)
Async XLA Ops:
  3.5 18.9 %collective-permute-start = (bf16[8,640,128]{2,1,0:T(8,128)(2,1)S(1)}, bf16[8,640,128]{2,1,0:T(8,128)(2,1)S(1)}, u32[]{:S(2)}, u32[]{:S(2)}) collective-permute-start(bf16[8,640,128]{2,1,0:T(8,128)(2,1)S(1)} %partial_send.1), channel_id=1, source_target_pairs={{0,16},{16,0},{1,17},{17,1},{2,18},{18,2},{3,19},{19,3},{4,20},{20... | collective-permute-start | bytes 3932168 | tf_op jit(solution)/shard_map/ppermute | solution.py:146
  43.0 31.6 %copy-start = (f32[40,4,8]{0,2,1:T(8,128)S(1)}, f32[40,4,8]{0,2,1:T(8,128)}, u32[]{:S(2)}) copy-start(f32[40,4,8]{0,2,1:T(8,128)} %param.7) | copy-start | bytes 15364
  43.0 31.6 %copy-start.1 = (f32[40,4,8]{0,2,1:T(8,128)S(1)}, f32[40,4,8]{0,2,1:T(8,128)}, u32[]{:S(2)}) copy-start(f32[40,4,8]{0,2,1:T(8,128)} %param.9) | copy-start | bytes 15364
  43.0 31.6 %copy-start.2 = (f32[40,4,8]{0,2,1:T(8,128)S(1)}, f32[40,4,8]{0,2,1:T(8,128)}, u32[]{:S(2)}) copy-start(f32[40,4,8]{0,2,1:T(8,128)} %param.8) | copy-start | bytes 15364

commit v6 on v5

--- a/solution.py
+++ b/solution.py
@@ -1,7 +1,9 @@
+import itertools
 import math
 
 import jax
 import jax.numpy as jnp
+import numpy as np
 from jax import lax
 from jax.experimental import pallas as pl
 from jax.experimental.pallas import tpu as pltpu
@@ -12,6 +14,7 @@
 HEAD = 128
 STEP = 8
 LANES = 128
+ALL_AXES = ("yh", "yl", "xh", "c", "zh", "zl", "xl")
 
 beta_first = 0.9
 beta_second = 0.95
@@ -137,6 +140,21 @@
     return (moment_one_new, moment_two_new, weights - learn_rate * update)
 
 
+def cubes(size):
+    shape = tuple(size(a) for a in ALL_AXES)
+    yh, yl, xh, cores, zh, zl, xl = shape
+    groups = []
+    for core, y0, z0, x0 in itertools.product(range(cores), range(yh), range(zh), range(xh)):
+        group = []
+        for py, pz, px in itertools.product(range(yl), range(zl), range(xl)):
+            y = (y0 + (core and py == 0)) % yh
+            z = (z0 + (core and pz == 0)) % zh
+            x = (x0 + (core and px == 0)) % xh
+            group.append(int(np.ravel_multi_index((y, py, x, core, z, pz, px), shape)))
+        groups.append(group)
+    return groups
+
+
 def shards(inputs, value_cotangent, master, first_moment, second_moment):
     fsdp = ("yh", "yl", "xh", "c")
     sizes = tuple(lax.axis_size(a) for a in ("zh", "zl", "xl", "yl", "xh"))
@@ -146,7 +164,9 @@
     arrived = lax.ppermute(outgoing, "c", [(0, 1), (1, 0)])
     kept = partials("keep", sizes, rows, core, inputs, value_cotangent)
     chip_sum = (kept + arrived.astype(jnp.float32)).astype(jnp.bfloat16)
-    parts = lax.all_to_all(chip_sum, ("yl", "zl", "xl"), 0, 0, tiled=True)
+    parts = lax.all_to_all(
+        chip_sum, ALL_AXES, 0, 0, axis_index_groups=cubes(lax.axis_size), tiled=True
+    )
     blocks = regroup(parts, sizes[0])
     peers = sizes[0] * lax.axis_size("yh") * lax.axis_size("xh")
     terms = lax.all_to_all(blocks.reshape(-1, 2, LANES), ("zh", "yh", "xh"), 0, 0, tiled=True)

time: 95.5 us -> 90.5 us (0.948)
  blocking collectives: 69.9 us -> 64.9 us
    all_to_all x1, blocking collectives: 30.8 us -> 23.3 us  [shards(): lax.all_to_all(blocks.reshape(-1, 2, LANES), ('zh', 'yh', 'xh'), 0, 0, ti...]
    all_to_all x1, blocking collectives: 20.3 us -> 24.7 us  [shards(): lax.all_to_all(chip_sum, ALL_AXES, 0, 0, axis_index_groups=cubes(lax.axis...]
    all_to_all x1, blocking collectives: 18.8 us -> 17 us  [shards(): arrived = lax.all_to_all(outgoing, fsdp, 0, 0, tiled=True)]
where the time goes in v6:
time: 90.5 us; the launch traced here: 90.2 us
  blocking collectives  64.9 us (72%)
  starting transfers between devices  16 us (18%)
  Pallas kernels  6.1 us (7%)
  local copies, waits for them, and re-layouts  1.37 us (2%)
  other arithmetic  1.07 us (1%)
    all_to_all x1, blocking collectives, shards(): lax.all_to_all(chip_sum, ALL_AXES, 0, 0, axis_index_groups=cubes(lax.axis...  24.7 us
    all_to_all x1, blocking collectives, shards(): lax.all_to_all(blocks.reshape(-1, 2, LANES), ('zh', 'yh', 'xh'), 0, 0, ti...  23.3 us
    all_to_all x1, blocking collectives, shards(): arrived = lax.all_to_all(outgoing, fsdp, 0, 0, tiled=True)  17 us
    ppermute x1, starting transfers between devices, shards(): arrived = lax.ppermute(outgoing, 'c', [(0, 1), (1, 0)])  16 us
    pallas_call x2, Pallas kernels, partials(): pl.pallas_call(lambda *refs: partial_kernel(sizes, rows, which, *refs), o...  5.73 us
  transfers between devices with their start and end apart: 1, of which 0 were waited for; matrix products, arithmetic and copies ran while one was open for 0% of the time, Pallas kernels for 3%

profile of v6, /device:TPU:1, one launch (start us, length us, event | category | flops | bytes accessed | tf_op | source)
XLA Modules:
  0.0 90.2 jit_solution(11994641525958323047)
XLA Ops:
  0.6 2.9 %partial_send.1 = bf16[8,640,128]{2,1,0:T(8,128)(2,1)S(1)} custom-call(s32[1]{0:T(128)} %bitcast.refs_0_, bf16[256,2560]{1,0:T(8,128)(2,1)} %refs_1_.3, bf16[256,512]{1,0:T(8,128)(2,1)} %refs_2_.3), custom_call_target="tpu_custom_call" | custom-call | flops 671088640 | bytes 3145728 | tf_op jit(solution)/shard_map/partial_send/pallas_call | solution.py:83
  3.5 16.0 %collective-permute-start = (bf16[8,640,128]{2,1,0:T(8,128)(2,1)S(1)}, bf16[8,640,128]{2,1,0:T(8,128)(2,1)S(1)}, u32[]{:S(2)}, u32[]{:S(2)}) collective-permute-start(bf16[8,640,128]{2,1,0:T(8,128)(2,1)S(1)} %partial_send.1), channel_id=1, source_target_pairs={{0,16},{16,0},{1,17},{17,1},{2,18},{18,2},{3,19},{19,3},{4,20},{20... | collective-permute-start | bytes 3932168 | tf_op jit(solution)/shard_map/ppermute | solution.py:164
  19.5 2.9 %partial_keep.1 = f32[8,640,128]{2,1,0:T(8,128)S(1)} custom-call(s32[1]{0:T(128)} %bitcast.refs_0_, bf16[256,2560]{1,0:T(8,128)(2,1)} %refs_1_.3, bf16[256,512]{1,0:T(8,128)(2,1)} %refs_2_.3), custom_call_target="tpu_custom_call" | custom-call | flops 671088640 | bytes 3145728 | tf_op jit(solution)/shard_map/partial_keep/pallas_call | solution.py:83
  22.4 0.0 collective-permute-done
  22.4 0.3 add_convert_fusion
  22.7 24.7 %all_to_all.15.refs_0_ = bf16[8,640,128]{2,1,0:T(8,128)(2,1)S(1)} all-to-all(bf16[8,640,128]{2,1,0:T(8,128)(2,1)S(1)} %add_convert_fusion), channel_id=1, replica_groups={{0,1,2,3,128,129,130,131},{32,33,34,35,160,161,162,163},{64,65,66,67,19..., dimensions={0} | all-to-all | bytes 2621440 | tf_op jit(solution)/shard_map/all_to_all | solution.py:167
  47.3 0.0 copy-start
  47.3 0.0 copy-start.1
  47.3 0.0 copy-start.2
  47.3 0.4 regroup.1
  47.7 23.3 %all_to_all.16 = bf16[320,2,128]{2,1,0:T(2,128)(2,1)S(1)} all-to-all(bf16[320,2,128]{2,1,0:T(2,128)(2,1)S(1)} %bitcast.11), channel_id=1, replica_groups=mesh['yh'=4,'yl'=2,'xh'=4,'c'=2,'zh'=4,'zl'=2,'xl'=2] {'zh','yh','xh'}, dimensions={0} | all-to-all | bytes 327680 | tf_op jit(solution)/shard_map/all_to_all | solution.py:172
  71.0 0.2 convert_reduce_fusion
  71.1 0.1 reshape.29
  71.3 0.1 copy.33
  71.4 0.0 copy-done
  71.4 0.0 copy-done.1
  71.4 0.0 copy-done.2
  71.4 0.6 convert_bitcast_fusion
  72.0 0.2 reshape.32
  72.2 17.0 %all_to_all.17 = bf16[64,2,160]{2,1,0:T(2,128)(2,1)S(1)} all-to-all(bf16[64,2,160]{2,1,0:T(2,128)(2,1)S(1)} %reshape.32), channel_id=1, replica_groups=mesh['yh'=4,'yl'=2,'xh'=4,'c'=2,'zh'=4,'zl'=2,'xl'=2] {'yh','yl','xh','c'}, dimensions={0} | all-to-all | bytes 81920 | tf_op jit(solution)/shard_map/all_to_all | solution.py:181
  89.2 0.1 reshape.33
  89.4 0.8 reshape.30
  (2 shorter events, 0.0 us)
Async XLA Ops:
  3.5 18.9 %collective-permute-start = (bf16[8,640,128]{2,1,0:T(8,128)(2,1)S(1)}, bf16[8,640,128]{2,1,0:T(8,128)(2,1)S(1)}, u32[]{:S(2)}, u32[]{:S(2)}) collective-permute-start(bf16[8,640,128]{2,1,0:T(8,128)(2,1)S(1)} %partial_send.1), channel_id=1, source_target_pairs={{0,16},{16,0},{1,17},{17,1},{2,18},{18,2},{3,19},{19,3},{4,20},{20... | collective-permute-start | bytes 3932168 | tf_op jit(solution)/shard_map/ppermute | solution.py:164
  47.3 24.0 %copy-start = (f32[40,4,8]{0,2,1:T(8,128)S(1)}, f32[40,4,8]{0,2,1:T(8,128)}, u32[]{:S(2)}) copy-start(f32[40,4,8]{0,2,1:T(8,128)} %param.7) | copy-start | bytes 15364
  47.3 24.0 %copy-start.1 = (f32[40,4,8]{0,2,1:T(8,128)S(1)}, f32[40,4,8]{0,2,1:T(8,128)}, u32[]{:S(2)}) copy-start(f32[40,4,8]{0,2,1:T(8,128)} %param.9) | copy-start | bytes 15364
  47.3 24.0 %copy-start.2 = (f32[40,4,8]{0,2,1:T(8,128)S(1)}, f32[40,4,8]{0,2,1:T(8,128)}, u32[]{:S(2)}) copy-start(f32[40,4,8]{0,2,1:T(8,128)} %param.8) | copy-start | bytes 15364

commit v7 on v6

--- a/solution.py
+++ b/solution.py
@@ -78,7 +78,7 @@
     tokens, d_in = x.shape
     blocks = math.prod(sizes[1:4])
     dtype = jnp.float32 if which == "keep" else jnp.bfloat16
-    chunk = 640
+    chunk = 1280
     anywhere = pl.BlockSpec(memory_space=pl.ANY)
     return pl.pallas_call(
         lambda *refs: partial_kernel(sizes, rows, which, *refs),

time: 90.5 us -> 90.4 us (level)
  transfers between devices with their start and end apart: 1 -> 1, of which waited for: 0 -> 1; matrix products, arithmetic and copies ran while one was open for 0% -> 0% of each run, Pallas kernels for 3% -> 3%
where the time goes in v7:
time: 90.4 us; the launch traced here: 90.1 us
  blocking collectives  65.4 us (72%)
  starting transfers between devices  16 us (18%)
  Pallas kernels  5.33 us (6%)
  local copies, waits for them, and re-layouts  1.37 us (2%)
  other arithmetic  1.07 us (1%)
    all_to_all x1, blocking collectives, shards(): lax.all_to_all(chip_sum, ALL_AXES, 0, 0, axis_index_groups=cubes(lax.axis...  24.7 us
    all_to_all x1, blocking collectives, shards(): lax.all_to_all(blocks.reshape(-1, 2, LANES), ('zh', 'yh', 'xh'), 0, 0, ti...  23.6 us
    all_to_all x1, blocking collectives, shards(): arrived = lax.all_to_all(outgoing, fsdp, 0, 0, tiled=True)  17.2 us
    ppermute x1, starting transfers between devices, shards(): arrived = lax.ppermute(outgoing, 'c', [(0, 1), (1, 0)])  16 us
    pallas_call x2, Pallas kernels, partials(): pl.pallas_call(lambda *refs: partial_kernel(sizes, rows, which, *refs), o...  4.96 us
  transfers between devices with their start and end apart: 1, of which 1 were waited for; matrix products, arithmetic and copies ran while one was open for 0% of the time, Pallas kernels for 3%

profile of v7, /device:TPU:1, one launch (start us, length us, event | category | flops | bytes accessed | tf_op | source)
XLA Modules:
  0.0 90.1 jit_solution(16274020986669494254)
XLA Ops:
  0.6 2.5 %partial_send.1 = bf16[8,640,128]{2,1,0:T(8,128)(2,1)S(1)} custom-call(s32[1]{0:T(128)} %bitcast.refs_0_, bf16[256,2560]{1,0:T(8,128)(2,1)} %refs_1_.3, bf16[256,512]{1,0:T(8,128)(2,1)} %refs_2_.3), custom_call_target="tpu_custom_call" | custom-call | flops 671088640 | bytes 3145728 | tf_op jit(solution)/shard_map/partial_send/pallas_call | solution.py:83
  3.1 16.0 %collective-permute-start = (bf16[8,640,128]{2,1,0:T(8,128)(2,1)S(1)}, bf16[8,640,128]{2,1,0:T(8,128)(2,1)S(1)}, u32[]{:S(2)}, u32[]{:S(2)}) collective-permute-start(bf16[8,640,128]{2,1,0:T(8,128)(2,1)S(1)} %partial_send.1), channel_id=1, source_target_pairs={{0,16},{16,0},{1,17},{17,1},{2,18},{18,2},{3,19},{19,3},{4,20},{20... | collective-permute-start | bytes 3932168 | tf_op jit(solution)/shard_map/ppermute | solution.py:164
  19.1 2.5 %partial_keep.1 = f32[8,640,128]{2,1,0:T(8,128)S(1)} custom-call(s32[1]{0:T(128)} %bitcast.refs_0_, bf16[256,2560]{1,0:T(8,128)(2,1)} %refs_1_.3, bf16[256,512]{1,0:T(8,128)(2,1)} %refs_2_.3), custom_call_target="tpu_custom_call" | custom-call | flops 671088640 | bytes 3145728 | tf_op jit(solution)/shard_map/partial_keep/pallas_call | solution.py:83
  21.6 0.1 collective-permute-done
  21.8 0.3 add_convert_fusion
  22.0 24.7 %all_to_all.15.refs_0_ = bf16[8,640,128]{2,1,0:T(8,128)(2,1)S(1)} all-to-all(bf16[8,640,128]{2,1,0:T(8,128)(2,1)S(1)} %add_convert_fusion), channel_id=1, replica_groups={{0,1,2,3,128,129,130,131},{32,33,34,35,160,161,162,163},{64,65,66,67,19..., dimensions={0} | all-to-all | bytes 2621440 | tf_op jit(solution)/shard_map/all_to_all | solution.py:167
  46.7 0.0 copy-start
  46.7 0.0 copy-start.1
  46.7 0.0 copy-start.2
  46.7 0.4 regroup.1
  47.1 23.6 %all_to_all.16 = bf16[320,2,128]{2,1,0:T(2,128)(2,1)S(1)} all-to-all(bf16[320,2,128]{2,1,0:T(2,128)(2,1)S(1)} %bitcast.11), channel_id=1, replica_groups=mesh['yh'=4,'yl'=2,'xh'=4,'c'=2,'zh'=4,'zl'=2,'xl'=2] {'zh','yh','xh'}, dimensions={0} | all-to-all | bytes 327680 | tf_op jit(solution)/shard_map/all_to_all | solution.py:172
  70.7 0.2 convert_reduce_fusion
  70.8 0.1 reshape.29
  71.0 0.1 copy.33
  71.1 0.0 copy-done
  71.1 0.0 copy-done.1
  71.1 0.0 copy-done.2
  71.1 0.6 convert_bitcast_fusion
  71.7 0.2 reshape.32
  71.9 17.2 %all_to_all.17 = bf16[64,2,160]{2,1,0:T(2,128)(2,1)S(1)} all-to-all(bf16[64,2,160]{2,1,0:T(2,128)(2,1)S(1)} %reshape.32), channel_id=1, replica_groups=mesh['yh'=4,'yl'=2,'xh'=4,'c'=2,'zh'=4,'zl'=2,'xl'=2] {'yh','yl','xh','c'}, dimensions={0} | all-to-all | bytes 81920 | tf_op jit(solution)/shard_map/all_to_all | solution.py:181
  89.1 0.1 reshape.33
  89.3 0.8 reshape.30
  (2 shorter events, 0.0 us)
Async XLA Ops:
  3.1 18.7 %collective-permute-start = (bf16[8,640,128]{2,1,0:T(8,128)(2,1)S(1)}, bf16[8,640,128]{2,1,0:T(8,128)(2,1)S(1)}, u32[]{:S(2)}, u32[]{:S(2)}) collective-permute-start(bf16[8,640,128]{2,1,0:T(8,128)(2,1)S(1)} %partial_send.1), channel_id=1, source_target_pairs={{0,16},{16,0},{1,17},{17,1},{2,18},{18,2},{3,19},{19,3},{4,20},{20... | collective-permute-start | bytes 3932168 | tf_op jit(solution)/shard_map/ppermute | solution.py:164
  46.7 24.4 %copy-start = (f32[40,4,8]{0,2,1:T(8,128)S(1)}, f32[40,4,8]{0,2,1:T(8,128)}, u32[]{:S(2)}) copy-start(f32[40,4,8]{0,2,1:T(8,128)} %param.7) | copy-start | bytes 15364
  46.7 24.4 %copy-start.1 = (f32[40,4,8]{0,2,1:T(8,128)S(1)}, f32[40,4,8]{0,2,1:T(8,128)}, u32[]{:S(2)}) copy-start(f32[40,4,8]{0,2,1:T(8,128)} %param.9) | copy-start | bytes 15364
  46.7 24.4 %copy-start.2 = (f32[40,4,8]{0,2,1:T(8,128)S(1)}, f32[40,4,8]{0,2,1:T(8,128)}, u32[]{:S(2)}) copy-start(f32[40,4,8]{0,2,1:T(8,128)} %param.8) | copy-start | bytes 15364
